TPU v7x, 512 devices: a whole 4x4x16 slice. The times are simulated.
512 devices in a mesh: tok: 8 (over x, core), vocab: 64 (over z, y).
Axes of the slice: x: 4, y: 4, z: 16, core: 2. Of those that a mesh axis runs over, the one named last changes fastest.
Arguments:
- hidden: bfloat16 [6144, 4096], P('tok', 'vocab'), as said below
- weight: bfloat16 [4096, 65536], P('tok', 'vocab'), may hold values from -0.09375 to 0.09375
- targets: int32 [6144], P('tok'), may hold values from 0 to 65535
- domains: int32 [6144], P('tok'), may hold values from 0 to 63
- seq_len: int32 [48], P('tok'), may hold values from 1 to 128
Outputs:
- token_loss: float32 [6144], P(('tok', 'vocab'))
- domain_mean: float32 [64], replicated
Inputs may be any that keep to these rules, and one draw needn't show every extreme that they name: hidden states of the eval window.
All inputs are finite; a program needn't handle non-finite values.
Results may differ from a plain program's by a relative error of at most 0.0003.
Values may be sent and summed in bfloat16 or wider, within the bound.
No kernel may reach another device: no remote copies, remote signals or barrier semaphores. Data moves between devices by JAX's collectives and lax.ppermute only.
A program may use at most 64 MiB of HBM per device.

v0:
```python
import jax
import jax.numpy as jnp
from jax import lax
from jax.sharding import Mesh
from jax.sharding import PartitionSpec as P

SEQ_LEN = 128
DOMAINS = 64
TOK = ("x", "c")
VOCAB = ("z", "y")
SWAP = [(0, 1), (1, 0)]


def to_all(array, axis, copies):
    return lax.all_to_all(
        jnp.broadcast_to(array[None], (copies, *array.shape)), axis, 0, 0, tiled=True
    )


def gathered_weight(weight):
    core = lax.axis_index("c")
    half = weight.shape[1] // 2
    keep = lax.dynamic_slice_in_dim(weight, core * half, half, 1)
    give = lax.dynamic_slice_in_dim(weight, (1 - core) * half, half, 1)
    other = lax.ppermute(give, "c", SWAP)
    rows = jnp.where(
        core == 0, jnp.concatenate([keep, other], 0), jnp.concatenate([other, keep], 0)
    )
    chips = lax.axis_size("x")
    own = to_all(rows, "x", chips).reshape(chips * rows.shape[0], half)
    return (own, lax.ppermute(own, "c", SWAP))


def tail(lse, picked, domains, seq_len):
    tokens = lse.shape[0]
    zs, ys = (lax.axis_size("z"), lax.axis_size("y"))
    own = tokens // (zs * ys)
    y = lax.axis_index("y")
    slices = jnp.stack([lse, picked]).reshape(2, zs, ys, own).transpose(2, 0, 1, 3)
    send = jnp.broadcast_to(slices.reshape(1, ys, -1), (zs, ys, 2 * zs * own))
    got = lax.all_to_all(send.reshape(zs * ys, -1), VOCAB, 0, 0, tiled=True)
    got = got.reshape(zs * ys, 2, zs * own)
    top = jnp.max(got[:, 0], axis=0)
    total = jnp.sum(jnp.exp(got[:, 0] - top[None]), axis=0)
    raw = jnp.log(total) + top - jnp.sum(got[:, 1], axis=0)
    index = lax.iota(jnp.int32, zs * own)
    local = index // own * (ys * own) + y * own + index % own
    seqs = seq_len.shape[0]
    lengths = jnp.sum(
        jnp.where(
            (local // SEQ_LEN)[:, None] == lax.broadcasted_iota(jnp.int32, (zs * own, seqs), 1),
            seq_len[None],
            0,
        ),
        axis=1,
    )
    mask = (local % SEQ_LEN < lengths).astype(jnp.float32)
    loss = raw * mask
    domain = lax.dynamic_index_in_dim(domains.reshape(zs, ys, own), y, 1, False).reshape(-1)
    here = domain[None, :] == lax.broadcasted_iota(jnp.int32, (DOMAINS, zs * own), 0)
    sums = jnp.sum(jnp.where(here, loss[None], 0.0), axis=1)
    counts = jnp.sum(jnp.where(here, mask[None], 0.0), axis=1)
    part = jnp.concatenate([sums, counts])
    axes = ("x", "c", "y")
    whole = jnp.sum(to_all(part, axes, lax.axis_size(axes)), axis=0)
    mean = whole[:DOMAINS] / jnp.maximum(whole[DOMAINS:], 1.0)
    token_loss = lax.dynamic_index_in_dim(loss.reshape(zs, own), lax.axis_index("z"), 0, False)
    return (token_loss, mean)


def body(hidden, weight, targets, domains, seq_len):
    features = lax.all_gather(hidden, "y", axis=1, tiled=True)
    features = lax.all_gather(features, "z", axis=1, tiled=True)
    core = lax.axis_index("c")
    halves = gathered_weight(weight)
    columns = weight.shape[1]
    half = columns // 2
    first = lax.axis_index(VOCAB) * columns
    logits = [jnp.dot(features, w, preferred_element_type=jnp.float32) for w in halves]
    tops = jnp.maximum(jnp.max(logits[0], axis=1), jnp.max(logits[1], axis=1))
    total, picked = (0.0, 0.0)
    for values, start in zip(logits, (core * half, (1 - core) * half)):
        ids = first + start + lax.broadcasted_iota(jnp.int32, values.shape, 1)
        total += jnp.sum(jnp.exp(values - tops[:, None]), axis=1)
        picked += jnp.sum(jnp.where(ids == targets[:, None], values, 0.0), axis=1)
    return tail(jnp.log(total) + tops, picked, domains, seq_len)


def solution(mesh):
    split = Mesh(mesh.devices.reshape(4, 2, 16, 4), ("x", "c", "z", "y"))
    placed = (P(TOK, VOCAB), P(TOK, VOCAB), P(TOK), P(TOK), P(TOK))
    return jax.shard_map(
        body, mesh=split, in_specs=placed, out_specs=(P((*TOK, *VOCAB)), P()), check_vma=False
    )
```

profile of v0, /device:TPU:1, one launch (start us, length us, event | category | flops | bytes accessed | tf_op | source)
XLA Modules:
  0.0 175.8 jit_solution(721808868574512698)
XLA Ops:
  7.2 0.0 all-gather.2.cloned.1.call-start
  7.2 13.0 %all_gather.6 = bf16[768,256]{0,1:T(8,128)(2,1)} all-gather(bf16[768,64]{0,1:T(8,128)(2,1)} %param.5), channel_id=1, replica_groups=mesh['x'=4,'c'=2,'z'=16,'y'=4] {'y'}, dimensions={1}, use_global_device_ids=true | all-gather | bytes 491520 | tf_op jit(solution)/shard_map/all_gather | solution.py:72
  20.2 0.0 all-gather.2.cloned.1.call-update
  20.2 1.3 constant_dynamic-slice_fusion.6
  21.5 9.2 %collective-permute-start = (bf16[512,512]{1,0:T(8,128)(2,1)S(1)}, bf16[512,512]{1,0:T(8,128)(2,1)S(1)}, u32[]{:S(2)}, u32[]{:S(2)}) collective-permute-start(bf16[512,512]{1,0:T(8,128)(2,1)S(1)} %get-tuple-element.17), channel_id=1, source_target_pairs={{0,64},{64,0},{1,65},{65,1},{2,66},{66,2},{3,67},{67,3},{4,68},{68... | collective-permute-start | bytes 1572872 | tf_op jit(solution)/shard_map/ppermute | solution.py:25
  30.7 1.5 collective-permute-done
  32.3 0.5 maximum_select_fusion
  32.7 0.3 broadcast_in_dim.65
  33.1 0.0 copy-start.2
  33.1 51.9 %all_to_all.20 = bf16[4,1024,512]{2,1,0:T(8,128)(2,1)} all-to-all(bf16[4,1024,512]{2,1,0:T(8,128)(2,1)S(1)} %broadcast_in_dim.65), channel_id=1, replica_groups=mesh['x'=4,'c'=2,'z'=16,'y'=4] {'x'}, dimensions={0} | all-to-all | bytes 8388608 | tf_op jit(solution)/shard_map/all_to_all | solution.py:15
  85.0 3.1 %collective-permute-start.1 = (bf16[4096,512]{1,0:T(8,128)(2,1)}, bf16[4096,512]{1,0:T(8,128)(2,1)}, u32[]{:S(2)}, u32[]{:S(2)}) collective-permute-start(bf16[4096,512]{1,0:T(8,128)(2,1)} %bitcast), channel_id=1, source_target_pairs={{0,64},{64,0},{1,65},{65,1},{2,66},{66,2},{3,67},{67,3},{4,68},{68... | collective-permute-start | bytes 12582920 | tf_op jit(solution)/shard_map/ppermute | solution.py:31
  88.2 0.0 copy-done.2
  88.2 0.1 select_reduce_fusion.2
  88.3 20.7 %all-gather.2.cloned.1.call-done = bf16[768,4096]{0,1:T(8,128)(2,1)} async-done(((bf16[768,256]{0,1:T(8,128)(2,1)}), bf16[768,4096]{0,1:T(8,128)(2,1)}) %all-gather.2.cloned.1.call-update) | async-done | bytes 6291472 | tf_op jit(solution)/shard_map/all_gather | solution.py:73
  109.0 0.0 copy-start.3
  109.0 7.4 %fusion.28 = (f32[768]{0:T(1024)S(1)}, f32[512,768]{1,0:T(8,128)S(1)}) fusion(bf16[4096,512]{1,0:T(8,128)(2,1)} %bitcast, bf16[768,4096]{0,1:T(8,128)(2,1)} %all-gather.2.cloned.1.call-done), kind=kOutput, calls=%fused_computation.76 | convolution fusion | flops 3221617920 | bytes 12061696 | tf_op jit(solution)/shard_map/dot_general | solution.py:79
  116.5 0.0 copy-start
  116.5 0.0 collective-permute-done.1
  116.5 0.0 copy-done.3
  116.5 5.3 %fusion.29 = (f32[768]{0:T(1024)S(1)}, f32[512,768]{1,0:T(8,128)S(1)}) fusion(bf16[4096,512]{1,0:T(8,128)(2,1)} %collective-permute-done.1, bf16[768,4096]{0,1:T(8,128)(2,1)S(1)} %copy-done.3), kind=kOutput, calls=%fused_computation.77 | convolution fusion | flops 3221617920 | bytes 12061696 | tf_op jit(solution)/shard_map/dot_general | solution.py:79
  121.8 0.0 copy-start.1
  121.8 0.0 copy-done
  121.8 0.8 fusion.4
  122.6 0.1 add.194
  122.7 0.1 add.203
  122.9 0.1 broadcast_in_dim.67
  123.0 0.7 all_to_all.14
  123.8 13.5 %all-to-all-start.1 = ((f32[64,1,384]{2,1,0:T(1,128)}), f32[64,1,384]{2,1,0:T(1,128)S(1)}, u32[]{:S(2)}, u32[]{:S(2)}) async-start(f32[64,1,384]{2,1,0:T(1,128)} %all_to_all.14), calls=%async_computation.1 | async-start | bytes 196608 | tf_op jit(solution)/shard_map/all_to_all | solution.py:41
  137.2 0.0 copy-done.1
  137.3 0.1 reshape.234
  137.4 0.1 eq.44
  137.5 0.1 reduce_sum.93
  137.6 14.1 %all-to-all-done.1 = f32[64,1,384]{2,1,0:T(1,128)S(1)} async-done(((f32[64,1,384]{2,1,0:T(1,128)}), f32[64,1,384]{2,1,0:T(1,128)S(1)}, u32[]{:S(2)}, u32[]{:S(2)}) %all-to-all-start.1) | async-done | bytes 98336 | tf_op jit(solution)/shard_map/all_to_all | solution.py:41
  151.7 0.2 reduce.5
  152.0 0.1 reshape.233
  152.1 0.2 slice_reduce_fusion.1
  152.3 0.1 select_reduce_fusion.1
  152.4 0.1 pad_maximum_fusion
  152.5 0.6 broadcast_in_dim.72
  153.1 8.3 %all-to-all-start.2 = ((f32[32,1,128]{2,1,0:T(1,128)}), f32[32,1,128]{2,1,0:T(1,128)S(1)}, u32[]{:S(2)}, u32[]{:S(2)}) async-start(f32[32,1,128]{2,1,0:T(1,128)} %broadcast_in_dim.72), calls=%async_computation.2 | async-start | bytes 32768 | tf_op jit(solution)/shard_map/all_to_all | solution.py:15
  161.4 0.1 sub.59
  161.5 0.5 fusion.25
  162.1 6.3 %all-to-all-done.2 = f32[32,1,128]{2,1,0:T(1,128)S(1)} async-done(((f32[32,1,128]{2,1,0:T(1,128)}), f32[32,1,128]{2,1,0:T(1,128)S(1)}, u32[]{:S(2)}, u32[]{:S(2)}) %all-to-all-start.2) | async-done | bytes 16416 | tf_op jit(solution)/shard_map/all_to_all | solution.py:15
  168.4 0.6 maximum_divide_fusion
  (15 shorter events, 0.3 us)
Async XLA Ops:
  7.2 101.9 %all-gather.2.cloned.1.call-start = ((), (), s32[]{:S(2)}) async-start(), calls=%async_computation.3 | async-start | bytes 6684672 | tf_op jit(solution)/shard_map/all_gather | solution.py:73
  21.5 10.7 %collective-permute-start = (bf16[512,512]{1,0:T(8,128)(2,1)S(1)}, bf16[512,512]{1,0:T(8,128)(2,1)S(1)}, u32[]{:S(2)}, u32[]{:S(2)}) collective-permute-start(bf16[512,512]{1,0:T(8,128)(2,1)S(1)} %get-tuple-element.17), channel_id=1, source_target_pairs={{0,64},{64,0},{1,65},{65,1},{2,66},{66,2},{3,67},{67,3},{4,68},{68... | collective-permute-start | bytes 1572872 | tf_op jit(solution)/shard_map/ppermute | solution.py:25
  33.1 55.1 %copy-start.2 = (s32[6]{0:T(128)S(1)}, s32[6]{0:T(128)}, u32[]{:S(2)}) copy-start(s32[6]{0:T(128)} %param.9) | copy-start | bytes 76
  85.0 31.5 %collective-permute-start.1 = (bf16[4096,512]{1,0:T(8,128)(2,1)}, bf16[4096,512]{1,0:T(8,128)(2,1)}, u32[]{:S(2)}, u32[]{:S(2)}) collective-permute-start(bf16[4096,512]{1,0:T(8,128)(2,1)} %bitcast), channel_id=1, source_target_pairs={{0,64},{64,0},{1,65},{65,1},{2,66},{66,2},{3,67},{67,3},{4,68},{68... | collective-permute-start | bytes 12582920 | tf_op jit(solution)/shard_map/ppermute | solution.py:31
  109.0 7.4 %copy-start.3 = (bf16[768,4096]{0,1:T(8,128)(2,1)S(1)}, bf16[768,4096]{0,1:T(8,128)(2,1)}, u32[]{:S(2)}) copy-start(bf16[768,4096]{0,1:T(8,128)(2,1)} %all-gather.2.cloned.1.call-done) | copy-start | bytes 18874372
  116.5 5.4 %copy-start = (s32[768]{0:T(1024)S(1)}, s32[768]{0:T(1024)}, u32[]{:S(2)}) copy-start(s32[768]{0:T(1024)} %param.7) | copy-start | bytes 9220
  121.8 15.5 %copy-start.1 = (s32[768]{0:T(1024)S(1)}, s32[768]{0:T(1024)}, u32[]{:S(2)}) copy-start(s32[768]{0:T(1024)} %param.8) | copy-start | bytes 9220
  123.8 28.0 %all-to-all-start.1 = ((f32[64,1,384]{2,1,0:T(1,128)}), f32[64,1,384]{2,1,0:T(1,128)S(1)}, u32[]{:S(2)}, u32[]{:S(2)}) async-start(f32[64,1,384]{2,1,0:T(1,128)} %all_to_all.14), calls=%async_computation.1 | async-start | bytes 196608 | tf_op jit(solution)/shard_map/all_to_all | solution.py:41
  153.1 15.2 %all-to-all-start.2 = ((f32[32,1,128]{2,1,0:T(1,128)}), f32[32,1,128]{2,1,0:T(1,128)S(1)}, u32[]{:S(2)}, u32[]{:S(2)}) async-start(f32[32,1,128]{2,1,0:T(1,128)} %broadcast_in_dim.72), calls=%async_computation.2 | async-start | bytes 32768 | tf_op jit(solution)/shard_map/all_to_all | solution.py:15
Sparse Core Ops, SparseCore 0:
  20.3 88.6 all-gather.1
where the time goes:
time: 176 us
  blocking collectives  64.9 us (37%)
  waiting for transfers between devices  42.7 us (24%)
  starting transfers between devices  34.1 us (19%)
  between operations  14.3 us (8%)
  matrix products  12.7 us (7%)
  local copies, waits for them, and re-layouts  3.85 us (2%)
  other arithmetic  3.23 us (2%)
    all_to_all x1, blocking collectives, to_all(): lax.all_to_all(jnp.broadcast_to(array[None], (copies, *array.shape)), axi...  51.9 us
    all_gather x1, waiting for transfers between devices, body(): features = lax.all_gather(features, 'z', axis=1, tiled=True)  20.7 us
    all_to_all x1, waiting for transfers between devices, tail(): got = lax.all_to_all(send.reshape(zs * ys, -1), VOCAB, 0, 0, tiled=True)  14.1 us
    all_to_all x1, starting transfers between devices, tail(): got = lax.all_to_all(send.reshape(zs * ys, -1), VOCAB, 0, 0, tiled=True)  13.5 us
    all_gather x1, blocking collectives, body(): features = lax.all_gather(hidden, 'y', axis=1, tiled=True)  13 us
    dot_general x2, matrix products, body(): jnp.dot(features, w, preferred_element_type=jnp.float32)  12.7 us
    ppermute x1, starting transfers between devices, gathered_weight(): other = lax.ppermute(give, 'c', SWAP)  9.23 us
    all_to_all x1, starting transfers between devices, to_all(): lax.all_to_all(jnp.broadcast_to(array[None], (copies, *array.shape)), axi...  8.29 us
  transfers between devices with their start and end apart: 5, of which 4 were waited for; matrix products, arithmetic and copies ran while one was open for 6% of the time, Pallas kernels for 0%

commit v1 on v0

--- a/solution.py
+++ b/solution.py
@@ -70,7 +70,9 @@
 
 def body(hidden, weight, targets, domains, seq_len):
     features = lax.all_gather(hidden, "y", axis=1, tiled=True)
-    features = lax.all_gather(features, "z", axis=1, tiled=True)
+    features = jnp.concatenate(
+        lax.all_to_all(jnp.stack([features] * lax.axis_size("z")), "z", 0, 0), axis=1
+    )
     core = lax.axis_index("c")
     halves = gathered_weight(weight)
     columns = weight.shape[1]

time: 176 us -> 415 us (2.36)
  waiting for transfers between devices: 42.7 us -> 328 us
  blocking collectives: 64.9 us -> 10.8 us
  starting transfers between devices: 34.1 us -> 47.8 us
  between operations: 14.3 us -> 0.9 us
  local copies, waits for them, and re-layouts: 3.85 us -> 9.05 us
    all_to_all x0 -> x1, waiting for transfers between devices: none -> 268 us  [body(): lax.all_to_all(jnp.stack([features] * lax.axis_size('z')), 'z', 0, 0)]
    all_to_all x1 -> x0, blocking collectives: 51.9 us -> none  [to_all(): lax.all_to_all(jnp.broadcast_to(array[None], (copies, *array.shape)), axi...]
    all_to_all x1 -> x2, waiting for transfers between devices: 6.33 us -> 44.2 us  [to_all(): lax.all_to_all(jnp.broadcast_to(array[None], (copies, *array.shape)), axi...]
    all_gather x1 -> x0, waiting for transfers between devices: 20.7 us -> none  [body(): features = lax.all_gather(features, 'z', axis=1, tiled=True)]
    all_to_all x0 -> x1, starting transfers between devices: none -> 9.75 us  [body(): lax.all_to_all(jnp.stack([features] * lax.axis_size('z')), 'z', 0, 0)]
    all_to_all x1 -> x2, starting transfers between devices: 8.29 us -> 11.3 us  [to_all(): lax.all_to_all(jnp.broadcast_to(array[None], (copies, *array.shape)), axi...]
  transfers between devices with their start and end apart: 5 -> 6, of which waited for: 4 -> 5; matrix products, arithmetic and copies ran while one was open for 6% -> 2% of each run, Pallas kernels for 0% -> 0%
where the time goes in v1:
time: 415 us; the launch traced here: 414 us
  waiting for transfers between devices  328 us (79%)
  starting transfers between devices  47.8 us (12%)
  matrix products  14.2 us (3%)
  blocking collectives  10.8 us (3%)
  local copies, waits for them, and re-layouts  9.05 us (2%)
    all_to_all x1, waiting for transfers between devices, body(): lax.all_to_all(jnp.stack([features] * lax.axis_size('z')), 'z', 0, 0)  268 us
    all_to_all x2, waiting for transfers between devices, to_all(): lax.all_to_all(jnp.broadcast_to(array[None], (copies, *array.shape)), axi...  44.2 us
    all_to_all x1, starting transfers between devices, tail(): got = lax.all_to_all(send.reshape(zs * ys, -1), VOCAB, 0, 0, tiled=True)  14.6 us
    all_to_all x1, waiting for transfers between devices, tail(): got = lax.all_to_all(send.reshape(zs * ys, -1), VOCAB, 0, 0, tiled=True)  14.3 us
    dot_general x2, matrix products, body(): jnp.dot(features, w, preferred_element_type=jnp.float32)  14.2 us
    all_to_all x2, starting transfers between devices, to_all(): lax.all_to_all(jnp.broadcast_to(array[None], (copies, *array.shape)), axi...  11.3 us
    all_gather x1, blocking collectives, body(): features = lax.all_gather(hidden, 'y', axis=1, tiled=True)  10.8 us
    all_to_all x1, starting transfers between devices, body(): lax.all_to_all(jnp.stack([features] * lax.axis_size('z')), 'z', 0, 0)  9.75 us
  transfers between devices with their start and end apart: 6, of which 5 were waited for; matrix products, arithmetic and copies ran while one was open for 2% of the time, Pallas kernels for 0%

profile of v1, /device:TPU:1, one launch (start us, length us, event | category | flops | bytes accessed | tf_op | source)
XLA Modules:
  0.0 414.2 jit_solution(9382721074768436457)
XLA Ops:
  0.6 1.3 constant_dynamic-slice_fusion.6
  1.9 8.7 %collective-permute-start = (bf16[512,512]{1,0:T(8,128)(2,1)S(1)}, bf16[512,512]{1,0:T(8,128)(2,1)S(1)}, u32[]{:S(2)}, u32[]{:S(2)}) collective-permute-start(bf16[512,512]{1,0:T(8,128)(2,1)S(1)} %get-tuple-element.17), channel_id=1, source_target_pairs={{0,64},{64,0},{1,65},{65,1},{2,66},{66,2},{3,67},{67,3},{4,68},{68... | collective-permute-start | bytes 1572872 | tf_op jit(solution)/shard_map/ppermute | solution.py:25
  10.7 1.5 collective-permute-done
  12.2 0.5 maximum_select_fusion
  12.6 2.2 broadcast_in_dim.65
  14.9 0.0 copy-start
  14.9 5.1 %all-to-all-start = ((bf16[4,1024,512]{2,1,0:T(8,128)(2,1)}), bf16[4,1024,512]{2,1,0:T(8,128)(2,1)}, u32[]{:S(2)}, u32[]{:S(2)}) async-start(bf16[4,1024,512]{2,1,0:T(8,128)(2,1)} %broadcast_in_dim.65), calls=%async_computation | async-start | bytes 8388608 | tf_op jit(solution)/shard_map/all_to_all | solution.py:15
  20.0 0.0 copy-done
  20.0 10.8 %all_gather.3 = bf16[768,256]{0,1:T(8,128)(2,1)S(1)} all-gather(bf16[768,64]{0,1:T(8,128)(2,1)S(1)} %copy-done), channel_id=1, replica_groups=mesh['x'=4,'c'=2,'z'=16,'y'=4] {'y'}, dimensions={1}, use_global_device_ids=true | all-gather | bytes 491520 | tf_op jit(solution)/shard_map/all_gather | solution.py:72
  30.8 37.7 %all-to-all-done = bf16[4,1024,512]{2,1,0:T(8,128)(2,1)} async-done(((bf16[4,1024,512]{2,1,0:T(8,128)(2,1)}), bf16[4,1024,512]{2,1,0:T(8,128)(2,1)}, u32[]{:S(2)}, u32[]{:S(2)}) %all-to-all-start) | async-done | bytes 4194336 | tf_op jit(solution)/shard_map/all_to_all | solution.py:15
  68.5 3.3 stack.4
  71.8 0.0 copy-start.3
  71.8 9.7 %all-to-all-start.1 = ((bf16[16,768,256]{1,2,0:T(8,128)(2,1)}), bf16[16,768,256]{1,2,0:T(8,128)(2,1)}, u32[]{:S(2)}, u32[]{:S(2)}) async-start(bf16[16,768,256]{1,2,0:T(8,128)(2,1)} %stack.4), calls=%async_computation.1 | async-start | bytes 12582912 | tf_op jit(solution)/shard_map/all_to_all | solution.py:74
  81.6 3.4 collective-permute-start.1
  85.0 0.0 copy-done.3
  85.1 0.1 select_reduce_fusion.2
  85.1 268.2 %all-to-all-done.1 = bf16[16,768,256]{1,2,0:T(8,128)(2,1)} async-done(((bf16[16,768,256]{1,2,0:T(8,128)(2,1)}), bf16[16,768,256]{1,2,0:T(8,128)(2,1)}, u32[]{:S(2)}, u32[]{:S(2)}) %all-to-all-start.1) | async-done | bytes 6291488 | tf_op jit(solution)/shard_map/all_to_all | solution.py:74
  353.3 7.1 %fusion.28 = (f32[768]{0:T(1024)S(1)}, f32[512,768]{1,0:T(8,128)S(1)}) fusion(bf16[4096,512]{1,0:T(8,128)(2,1)} %bitcast, bf16[768,4096]{0,1:T(8,128)(2,1)} %bitcast.2), kind=kOutput, calls=%fused_computation.76 | convolution fusion | flops 3221617920 | bytes 12061696 | tf_op jit(solution)/shard_map/dot_general | solution.py:81
  360.4 0.0 copy-start.1
  360.4 0.0 collective-permute-done.1
  360.4 7.1 %fusion.29 = (f32[768]{0:T(1024)S(1)}, f32[512,768]{1,0:T(8,128)S(1)}) fusion(bf16[4096,512]{1,0:T(8,128)(2,1)} %collective-permute-done.1, bf16[768,4096]{0,1:T(8,128)(2,1)} %bitcast.2), kind=kOutput, calls=%fused_computation.77 | convolution fusion | flops 3221617920 | bytes 12061696 | tf_op jit(solution)/shard_map/dot_general | solution.py:81
  367.6 0.0 copy-start.2
  367.6 0.0 copy-done.1
  367.6 0.8 fusion.4
  368.4 0.1 add.203
  368.5 0.1 add.194
  368.7 0.1 broadcast_in_dim.67
  368.8 0.7 all_to_all.18
  369.5 14.6 %all-to-all-start.2 = ((f32[64,1,384]{2,1,0:T(1,128)}), f32[64,1,384]{2,1,0:T(1,128)S(1)}, u32[]{:S(2)}, u32[]{:S(2)}) async-start(f32[64,1,384]{2,1,0:T(1,128)} %all_to_all.18), calls=%async_computation.2 | async-start | bytes 196608 | tf_op jit(solution)/shard_map/all_to_all | solution.py:41
  384.2 0.1 reduce_sum.93
  384.3 0.0 copy-done.2
  384.3 0.1 reshape.244
  384.5 0.1 eq.44
  384.6 14.3 %all-to-all-done.2 = f32[64,1,384]{2,1,0:T(1,128)S(1)} async-done(((f32[64,1,384]{2,1,0:T(1,128)}), f32[64,1,384]{2,1,0:T(1,128)S(1)}, u32[]{:S(2)}, u32[]{:S(2)}) %all-to-all-start.2) | async-done | bytes 98336 | tf_op jit(solution)/shard_map/all_to_all | solution.py:41
  398.9 0.2 reduce.5
  399.2 0.1 reshape.243
  399.3 0.2 slice_reduce_fusion.1
  399.5 0.1 sub.59
  399.6 0.1 select_reduce_fusion.1
  399.7 0.1 pad_maximum_fusion
  399.8 0.6 broadcast_in_dim.72
  400.4 6.2 %all-to-all-start.3 = ((f32[32,1,128]{2,1,0:T(1,128)}), f32[32,1,128]{2,1,0:T(1,128)S(1)}, u32[]{:S(2)}, u32[]{:S(2)}) async-start(f32[32,1,128]{2,1,0:T(1,128)} %broadcast_in_dim.72), calls=%async_computation.3 | async-start | bytes 32768 | tf_op jit(solution)/shard_map/all_to_all | solution.py:15
  406.7 0.5 fusion.25
  407.2 6.4 %all-to-all-done.3 = f32[32,1,128]{2,1,0:T(1,128)S(1)} async-done(((f32[32,1,128]{2,1,0:T(1,128)}), f32[32,1,128]{2,1,0:T(1,128)S(1)}, u32[]{:S(2)}, u32[]{:S(2)}) %all-to-all-start.3) | async-done | bytes 16416 | tf_op jit(solution)/shard_map/all_to_all | solution.py:15
  413.6 0.6 maximum_divide_fusion
  (15 shorter events, 0.3 us)
Async XLA Ops:
  1.9 10.3 %collective-permute-start = (bf16[512,512]{1,0:T(8,128)(2,1)S(1)}, bf16[512,512]{1,0:T(8,128)(2,1)S(1)}, u32[]{:S(2)}, u32[]{:S(2)}) collective-permute-start(bf16[512,512]{1,0:T(8,128)(2,1)S(1)} %get-tuple-element.17), channel_id=1, source_target_pairs={{0,64},{64,0},{1,65},{65,1},{2,66},{66,2},{3,67},{67,3},{4,68},{68... | collective-permute-start | bytes 1572872 | tf_op jit(solution)/shard_map/ppermute | solution.py:25
  14.9 5.1 %copy-start = (bf16[768,64]{0,1:T(8,128)(2,1)S(1)}, bf16[768,64]{0,1:T(8,128)(2,1)}, u32[]{:S(2)}) copy-start(bf16[768,64]{0,1:T(8,128)(2,1)} %param.5) | copy-start | bytes 294916
  14.9 53.6 %all-to-all-start = ((bf16[4,1024,512]{2,1,0:T(8,128)(2,1)}), bf16[4,1024,512]{2,1,0:T(8,128)(2,1)}, u32[]{:S(2)}, u32[]{:S(2)}) async-start(bf16[4,1024,512]{2,1,0:T(8,128)(2,1)} %broadcast_in_dim.65), calls=%async_computation | async-start | bytes 8388608 | tf_op jit(solution)/shard_map/all_to_all | solution.py:15
  71.8 13.2 %copy-start.3 = (s32[6]{0:T(128)S(1)}, s32[6]{0:T(128)}, u32[]{:S(2)}) copy-start(s32[6]{0:T(128)} %param.9) | copy-start | bytes 76
  71.8 281.5 %all-to-all-start.1 = ((bf16[16,768,256]{1,2,0:T(8,128)(2,1)}), bf16[16,768,256]{1,2,0:T(8,128)(2,1)}, u32[]{:S(2)}, u32[]{:S(2)}) async-start(bf16[16,768,256]{1,2,0:T(8,128)(2,1)} %stack.4), calls=%async_computation.1 | async-start | bytes 12582912 | tf_op jit(solution)/shard_map/all_to_all | solution.py:74
  81.6 278.9 %collective-permute-start.1 = (bf16[4096,512]{1,0:T(8,128)(2,1)}, bf16[4096,512]{1,0:T(8,128)(2,1)}, u32[]{:S(2)}, u32[]{:S(2)}) collective-permute-start(bf16[4096,512]{1,0:T(8,128)(2,1)} %bitcast), channel_id=1, source_target_pairs={{0,64},{64,0},{1,65},{65,1},{2,66},{66,2},{3,67},{67,3},{4,68},{68... | collective-permute-start | bytes 12582920 | tf_op jit(solution)/shard_map/ppermute | solution.py:31
  360.4 7.2 %copy-start.1 = (s32[768]{0:T(1024)S(1)}, s32[768]{0:T(1024)}, u32[]{:S(2)}) copy-start(s32[768]{0:T(1024)} %param.7) | copy-start | bytes 9220
  367.6 16.7 %copy-start.2 = (s32[768]{0:T(1024)S(1)}, s32[768]{0:T(1024)}, u32[]{:S(2)}) copy-start(s32[768]{0:T(1024)} %param.8) | copy-start | bytes 9220
  369.5 29.4 %all-to-all-start.2 = ((f32[64,1,384]{2,1,0:T(1,128)}), f32[64,1,384]{2,1,0:T(1,128)S(1)}, u32[]{:S(2)}, u32[]{:S(2)}) async-start(f32[64,1,384]{2,1,0:T(1,128)} %all_to_all.18), calls=%async_computation.2 | async-start | bytes 196608 | tf_op jit(solution)/shard_map/all_to_all | solution.py:41
  400.4 13.2 %all-to-all-start.3 = ((f32[32,1,128]{2,1,0:T(1,128)}), f32[32,1,128]{2,1,0:T(1,128)S(1)}, u32[]{:S(2)}, u32[]{:S(2)}) async-start(f32[32,1,128]{2,1,0:T(1,128)} %broadcast_in_dim.72), calls=%async_computation.3 | async-start | bytes 32768 | tf_op jit(solution)/shard_map/all_to_all | solution.py:15
